TPU v7x, 32 devices: a whole 2x2x4 slice. The times are simulated.
32 devices in a mesh: mat: 4 (over x, core), frac: 8 (over z, y).
Axes of the slice: x: 2, y: 2, z: 4, core: 2. Of those that a mesh axis runs over, the one named last changes fastest.
Arguments:
- pressure_start: float32 [64, 512, 256], P('mat', 'frac'), may hold values from -6 to 6
- face_trans: float32 [3, 64, 512, 256], P(None, 'mat', 'frac'), may hold values from 0.2 to 2
- cell_coef: float32 [64, 512, 256], P('mat', 'frac'), may hold values from 0.05 to 0.5
- matrix_source: float32 [64, 512, 256], P('mat', 'frac'), may hold values from -6 to 6
- mortar_owner: int32 [16384, 1], P(('mat', 'frac')), may hold values from 0 to 31; in each aligned block of 512 rows (0 to 511, 512 to 1023, ...) at most 32 rows name the same one
- mortar_cell: int32 [16384], P(('mat', 'frac')), may hold values from 0 to 262143
- mortar_frac: int32 [16384], P(('mat', 'frac')), may hold values from 0 to 8191
- mortar_kappa: float32 [16384], P(('mat', 'frac')), may hold values from 0.5 to 2
- tiles: float32 [64, 4, 128, 128], P('frac'), may hold values from -0.25 to 0.25
- tile_cols: int32 [64, 4], P('frac'), may hold values from 0 to 63
- frac_diag: float32 [8192], P('frac'), may hold values from 4 to 8
- frac_source: float32 [8192], P('frac'), may hold values from -6 to 6
- fracture_start: float32 [8192], P('frac'), may hold values from -6 to 6
Outputs:
- pressure: float32 [64, 512, 256], P('mat', 'frac')
- fracture: float32 [8192], P('frac')
- flux: float32 [16384], P(('mat', 'frac'))
Inputs may be any that keep to these rules, and one draw needn't show every extreme that they name: `mortar_owner`: among the 512 mortar cells of one device, at most 32 name the same owner, and in some devices some owner is named exactly 32 times.
All inputs are finite; a program needn't handle non-finite values.
Results may differ from a plain program's by a relative error of at most 0.00015.
Values sent between devices are 32-bit elements; how exact they have to be, the bound alone decides.
A program may use at most 128 MiB of HBM per device.

v0:
```python
import jax
import jax.numpy as jnp
from jax import lax
from jax.sharding import PartitionSpec as P

SWEEPS = 2
CG_ITERS = 3
OUTER = 2
relax_weight = 0.8


def shifted(value, axis, steps):
    count = lax.axis_size(axis)
    leading, last = (max(0, -steps), min(count, count - steps))
    return lax.ppermute(value, axis, [(source, source + steps) for source in range(leading, last)])


def with_halo(block, sides, width):
    for axis, dim in sides:
        count = lax.axis_size(axis)
        forward = [(i, i + 1) for i in range(count - 1)]
        backward = [(target, source) for source, target in forward]
        low = lax.ppermute(
            lax.slice_in_dim(block, block.shape[dim] - width, None, axis=dim), axis, forward
        )
        high = lax.ppermute(lax.slice_in_dim(block, 0, width, axis=dim), axis, backward)
        block = jnp.concatenate([low, block, high], axis=dim)
    return block


def shift_next(values, along):
    padding = [(0, 0)] * values.ndim
    padding[along] = (0, 1)
    return lax.slice_in_dim(jnp.pad(values, padding), 1, values.shape[along] + 1, axis=along)


def shift_prev(values, along):
    padding = [(0, 0)] * values.ndim
    padding[along] = (1, 0)
    return lax.slice_in_dim(jnp.pad(values, padding), 0, values.shape[along], axis=along)


def relax(padded, coef_part, source_part, inside):
    centre = padded[1:-1, 1:-1]
    tx_here = coef_part[0, 1:-1, 1:-1]
    tx_low = coef_part[0, :-2, 1:-1]
    ty_here = coef_part[1, 1:-1, 1:-1]
    ty_low = coef_part[1, 1:-1, :-2]
    tz_here = coef_part[2, 1:-1, 1:-1]
    tz_low = shift_prev(tz_here, 2)
    cell_part = coef_part[3, 1:-1, 1:-1]
    base_part = coef_part[4, 1:-1, 1:-1]
    diagonal = cell_part + tx_here + tx_low + ty_here + ty_low + tz_here + tz_low
    diagonal = jnp.where(inside, diagonal, 1.0)
    applied = (
        diagonal * centre
        - tx_here * padded[2:, 1:-1]
        - tx_low * padded[:-2, 1:-1]
        - ty_here * padded[1:-1, 2:]
        - ty_low * padded[1:-1, :-2]
        - tz_here * shift_next(centre, 2)
        - tz_low * shift_prev(centre, 2)
    )
    updated = centre + relax_weight * (base_part + source_part - applied) / diagonal
    return jnp.where(inside, updated, 0.0)


def body(
    pressure_start,
    face_trans,
    cell_coef,
    matrix_source,
    mortar_owner,
    mortar_cell,
    mortar_frac,
    mortar_kappa,
    tiles,
    tile_cols,
    frac_diag,
    frac_source,
    fracture_start,
):
    width_x, width_y, depth_z = pressure_start.shape
    cells = width_x * width_y * depth_z
    mat_count = lax.axis_size("mat")
    frac_count = lax.axis_size("frac")
    devices = mat_count * frac_count
    row_mat = lax.axis_index("mat")
    row_frac = lax.axis_index("frac")
    size_b = tiles.shape[2]
    coefs = jnp.concatenate([face_trans, cell_coef[None], matrix_source[None]], 0)
    lower_x = shifted(face_trans[0, -1], "mat", 1)
    lower_y = shifted(face_trans[1, :, -1], "frac", 1)
    coef_ext = jnp.pad(coefs, ((0, 0), (1, 1), (1, 1), (0, 0)))
    coef_ext = coef_ext.at[0, 0, 1:-1].set(lower_x)
    coef_ext = coef_ext.at[1, 1:-1, 0].set(lower_y)
    owner = mortar_owner[:, 0]
    mortar_count = owner.shape[0]
    capacity = max(2, 2 * mortar_count // devices)
    hits = (owner[:, None] == jnp.arange(devices, dtype=jnp.int32)[None, :]).astype(jnp.int32)
    ranks = jnp.cumsum(hits, axis=0)
    slot = jnp.sum(ranks * hits, axis=1) - 1
    place = owner * capacity + slot
    index_slots = (
        jnp.full((devices * capacity,), cells, jnp.int32)
        .at[place]
        .set(mortar_cell)
        .reshape(devices, capacity)
    )
    asked = lax.all_to_all(index_slots, ("mat", "frac"), split_axis=0, concat_axis=0, tiled=True)
    asked_safe = jnp.minimum(asked, cells - 1)

    def fracture_apply(vector):
        whole = lax.all_gather(vector, "frac", axis=0, tiled=True)
        blocks = whole.reshape(-1, size_b)
        forward = jnp.einsum(
            "rtij,rtj->ri", tiles, blocks[tile_cols], precision=lax.Precision.HIGHEST
        )
        backward = jnp.einsum(
            "rtij,ri->rtj", tiles, vector.reshape(-1, size_b), precision=lax.Precision.HIGHEST
        )
        spread = jnp.zeros_like(blocks).at[tile_cols.reshape(-1)].add(backward.reshape(-1, size_b))
        returned = lax.psum_scatter(spread, "frac", scatter_dimension=0, tiled=True)
        return frac_diag * vector + 0.5 * (forward + returned).reshape(-1)

    def two_products(residual, image):
        return lax.psum((jnp.sum(residual * residual), jnp.sum(residual * image)), "frac")

    def solve_fracture(fracture, target):
        residual = target - fracture_apply(fracture)
        image = fracture_apply(residual)
        norm_now, product = two_products(residual, image)
        alpha = norm_now / product
        direction, along_image = (residual, image)
        for step in range(CG_ITERS):
            fracture = fracture + alpha * direction
            residual = residual - alpha * along_image
            if step + 1 < CG_ITERS:
                image = fracture_apply(residual)
                norm_next, product = two_products(residual, image)
                ratio = norm_next / norm_now
                alpha = norm_next / (product - ratio * norm_next / alpha)
                direction = residual + ratio * direction
                along_image = image + ratio * along_image
                norm_now = norm_next
        return fracture

    pressure = pressure_start
    fracture = fracture_start
    flux = jnp.zeros(mortar_kappa.shape, jnp.float32)
    for outer_no in range(OUTER):
        local_values = pressure.reshape(-1)[asked_safe]
        returned = lax.all_to_all(
            local_values, ("mat", "frac"), split_axis=0, concat_axis=0, tiled=True
        )
        trace = returned.reshape(-1)[place]
        fracture_whole = lax.all_gather(fracture, "frac", axis=0, tiled=True)
        flux = mortar_kappa * (trace - fracture_whole[mortar_frac])
        landed = jax.ops.segment_sum(flux, mortar_frac, num_segments=fracture_whole.shape[0])
        summed = lax.psum(landed, ("mat", "frac"))
        load = lax.dynamic_slice_in_dim(summed, row_frac * fracture.shape[0], fracture.shape[0])
        fracture = solve_fracture(fracture, frac_source + load)
        flux_slots = (
            jnp.zeros((devices * capacity,), jnp.float32)
            .at[place]
            .set(flux)
            .reshape(devices, capacity)
        )
        arrived = lax.all_to_all(
            flux_slots, ("mat", "frac"), split_axis=0, concat_axis=0, tiled=True
        )
        source = jax.ops.segment_sum(
            arrived.reshape(-1), asked_safe.reshape(-1), num_segments=cells
        ).reshape(pressure.shape)
        for sweep_no in range(SWEEPS):
            padded = with_halo(pressure, (("mat", 0), ("frac", 1)), 1)
            global_x = row_mat * width_x - 0 + jnp.arange(width_x)
            global_y = row_frac * width_y - 0 + jnp.arange(width_y)
            keep_x = (global_x >= 0) & (global_x < width_x * mat_count)
            keep_y = (global_y >= 0) & (global_y < width_y * frac_count)
            pressure = relax(
                padded, coef_ext, source, (keep_x[:, None] & keep_y[None, :])[:, :, None]
            )
    return (pressure, fracture, flux)


def solution(mesh):
    in_specs = (
        P("mat", "frac", None),
        P(None, "mat", "frac", None),
        P("mat", "frac", None),
        P("mat", "frac", None),
        P(("mat", "frac"), None),
        P(("mat", "frac")),
        P(("mat", "frac")),
        P(("mat", "frac")),
        P("frac", None, None, None),
        P("frac", None),
        P("frac"),
        P("frac"),
        P("frac"),
    )
    out_specs = (P("mat", "frac", None), P("frac"), P(("mat", "frac")))
    return jax.shard_map(body, mesh=mesh, in_specs=in_specs, out_specs=out_specs, check_vma=False)
```

profile of v0, /device:TPU:0, one launch (start us, length us, event | category | flops | bytes accessed | tf_op | source)
XLA Modules:
  0.0 977.3 jit_solution(13991142482101642097)
XLA Ops:
  30.5 31.1 %all_gather.26 = f32[8192]{0:T(1024)S(1)} all-gather(f32[1024]{0:T(1024)} %param.29), channel_id=1, replica_groups=mesh['mat'=4,'frac'=8] {'frac'}, dimensions={0}, use_global_device_ids=true | all-gather | bytes 36864 | tf_op jit(solution)/shard_map/all_gather | solution.py:157
  83.4 37.4 %all-reduce.10 = f32[64,128]{1,0:T(8,128)S(1)} all-reduce(f32[64,128]{1,0:T(8,128)S(1)} %scatter_custom_fusion.4), channel_id=2, replica_groups=mesh['mat'=4,'frac'=8] {'frac'}, use_global_device_ids=true, to_apply=%region_9.10.clone | all-reduce | flops 8192 | bytes 65536
  138.0 40.6 %psum.98 = f32[8192]{0:T(1024)S(1)} all-reduce(f32[8192]{0:T(1024)S(1)} %scatter_custom_fusion.3), channel_id=1, replica_groups=mesh['mat'=4,'frac'=8] {'mat','frac'}, use_global_device_ids=true, to_apply=%region_7.8 | all-reduce | flops 8192 | bytes 65536 | tf_op jit(solution)/shard_map/psum | solution.py:160
  178.7 30.8 %all_gather.27 = f32[8192]{0:T(1024)S(1)} all-gather(f32[1024]{0:T(1024)S(1)} %fusion.134), channel_id=1, replica_groups=mesh['mat'=4,'frac'=8] {'frac'}, dimensions={0}, use_global_device_ids=true | all-gather | bytes 36864 | tf_op jit(solution)/shard_map/all_gather | solution.py:114
  213.7 36.8 %all-reduce.11 = f32[64,128]{1,0:T(8,128)S(1)} all-reduce(f32[64,128]{1,0:T(8,128)S(1)} %scatter_custom_fusion.5), channel_id=3, replica_groups=mesh['mat'=4,'frac'=8] {'frac'}, use_global_device_ids=true, to_apply=%region_13.14.clone | all-reduce | flops 8192 | bytes 65536
  251.2 17.8 %all-reduce.23 = (f32[]{:T(128)}, f32[]{:T(128)}) all-reduce(f32[]{:T(128)} %get-tuple-element.38, f32[]{:T(128)} %get-tuple-element.37), channel_id=1, replica_groups=mesh['mat'=4,'frac'=8] {'frac'}, use_global_device_ids=true, to_apply=%region_11.12 | all-reduce | flops 2 | bytes 16 | tf_op jit(solution)/shard_map/psum | solution.py:127
  270.3 30.6 %all_gather.28 = f32[8192]{0:T(1024)S(1)} all-gather(f32[1024]{0:T(1024)S(1)} %multiply_subtract_fusion.3), channel_id=1, replica_groups=mesh['mat'=4,'frac'=8] {'frac'}, dimensions={0}, use_global_device_ids=true | all-gather | bytes 36864 | tf_op jit(solution)/shard_map/all_gather | solution.py:114
  305.1 34.9 %all-reduce.12 = f32[64,128]{1,0:T(8,128)S(1)} all-reduce(f32[64,128]{1,0:T(8,128)S(1)} %scatter_custom_fusion.6), channel_id=4, replica_groups=mesh['mat'=4,'frac'=8] {'frac'}, use_global_device_ids=true, to_apply=%region_19.20.clone | all-reduce | flops 8192 | bytes 65536
  340.7 17.8 %all-reduce.22 = (f32[]{:T(128)}, f32[]{:T(128)}) all-reduce(f32[]{:T(128)} %get-tuple-element.36, f32[]{:T(128)} %get-tuple-element.35), channel_id=1, replica_groups=mesh['mat'=4,'frac'=8] {'frac'}, use_global_device_ids=true, to_apply=%region_17.18 | all-reduce | flops 2 | bytes 16 | tf_op jit(solution)/shard_map/psum | solution.py:127
  362.9 30.6 %all_gather.29 = f32[8192]{0:T(1024)S(1)} all-gather(f32[1024]{0:T(1024)S(1)} %multiply_subtract_fusion.2), channel_id=1, replica_groups=mesh['mat'=4,'frac'=8] {'frac'}, dimensions={0}, use_global_device_ids=true | all-gather | bytes 36864 | tf_op jit(solution)/shard_map/all_gather | solution.py:114
  397.8 34.9 %all-reduce.13 = f32[64,128]{1,0:T(8,128)S(1)} all-reduce(f32[64,128]{1,0:T(8,128)S(1)} %scatter_custom_fusion.7), channel_id=5, replica_groups=mesh['mat'=4,'frac'=8] {'frac'}, use_global_device_ids=true, to_apply=%region_25.26.clone | all-reduce | flops 8192 | bytes 65536
  433.3 17.8 %all-reduce.21 = (f32[]{:T(128)}, f32[]{:T(128)}) all-reduce(f32[]{:T(128)} %get-tuple-element.34, f32[]{:T(128)} %get-tuple-element.33), channel_id=1, replica_groups=mesh['mat'=4,'frac'=8] {'frac'}, use_global_device_ids=true, to_apply=%region_23.24 | all-reduce | flops 2 | bytes 16 | tf_op jit(solution)/shard_map/psum | solution.py:127
  454.9 30.6 %all_gather.30 = f32[8192]{0:T(1024)S(1)} all-gather(f32[1024]{0:T(1024)S(1)} %multiply_add_fusion.1), channel_id=1, replica_groups=mesh['mat'=4,'frac'=8] {'frac'}, dimensions={0}, use_global_device_ids=true | all-gather | bytes 36864 | tf_op jit(solution)/shard_map/all_gather | solution.py:157
  530.4 37.6 %all-reduce.14 = f32[64,128]{1,0:T(8,128)S(1)} all-reduce(f32[64,128]{1,0:T(8,128)S(1)} %scatter_custom_fusion.11), channel_id=6, replica_groups=mesh['mat'=4,'frac'=8] {'frac'}, use_global_device_ids=true, to_apply=%region_33.34.clone | all-reduce | flops 8192 | bytes 65536
  608.3 41.0 %psum.105 = f32[8192]{0:T(1024)S(1)} all-reduce(f32[8192]{0:T(1024)S(1)} %scatter_custom_fusion.10), channel_id=1, replica_groups=mesh['mat'=4,'frac'=8] {'mat','frac'}, use_global_device_ids=true, to_apply=%region_31.32 | all-reduce | flops 8192 | bytes 65536 | tf_op jit(solution)/shard_map/psum | solution.py:160
  649.3 30.6 %all_gather.31 = f32[8192]{0:T(1024)S(1)} all-gather(f32[1024]{0:T(1024)S(1)} %fusion.119), channel_id=1, replica_groups=mesh['mat'=4,'frac'=8] {'frac'}, dimensions={0}, use_global_device_ids=true | all-gather | bytes 36864 | tf_op jit(solution)/shard_map/all_gather | solution.py:114
  684.3 36.9 %all-reduce.15 = f32[64,128]{1,0:T(8,128)S(1)} all-reduce(f32[64,128]{1,0:T(8,128)S(1)} %scatter_custom_fusion.12), channel_id=7, replica_groups=mesh['mat'=4,'frac'=8] {'frac'}, use_global_device_ids=true, to_apply=%region_37.38.clone | all-reduce | flops 8192 | bytes 65536
  721.9 17.8 %all-reduce.20 = (f32[]{:T(128)}, f32[]{:T(128)}) all-reduce(f32[]{:T(128)} %get-tuple-element.32, f32[]{:T(128)} %get-tuple-element.31), channel_id=1, replica_groups=mesh['mat'=4,'frac'=8] {'frac'}, use_global_device_ids=true, to_apply=%region_35.36 | all-reduce | flops 2 | bytes 16 | tf_op jit(solution)/shard_map/psum | solution.py:127
  741.0 30.6 %all_gather.32 = f32[8192]{0:T(1024)S(1)} all-gather(f32[1024]{0:T(1024)S(1)} %multiply_subtract_fusion.1), channel_id=1, replica_groups=mesh['mat'=4,'frac'=8] {'frac'}, dimensions={0}, use_global_device_ids=true | all-gather | bytes 36864 | tf_op jit(solution)/shard_map/all_gather | solution.py:114
  776.0 34.9 %all-reduce.16 = f32[64,128]{1,0:T(8,128)S(1)} all-reduce(f32[64,128]{1,0:T(8,128)S(1)} %scatter_custom_fusion.13), channel_id=8, replica_groups=mesh['mat'=4,'frac'=8] {'frac'}, use_global_device_ids=true, to_apply=%region_43.44.clone | all-reduce | flops 8192 | bytes 65536
  811.5 17.8 %all-reduce.19 = (f32[]{:T(128)}, f32[]{:T(128)}) all-reduce(f32[]{:T(128)} %get-tuple-element.30, f32[]{:T(128)} %get-tuple-element.29), channel_id=1, replica_groups=mesh['mat'=4,'frac'=8] {'frac'}, use_global_device_ids=true, to_apply=%region_41.42 | all-reduce | flops 2 | bytes 16 | tf_op jit(solution)/shard_map/psum | solution.py:127
  834.0 30.6 %all_gather.33 = f32[8192]{0:T(1024)S(1)} all-gather(f32[1024]{0:T(1024)S(1)} %multiply_subtract_fusion), channel_id=1, replica_groups=mesh['mat'=4,'frac'=8] {'frac'}, dimensions={0}, use_global_device_ids=true | all-gather | bytes 36864 | tf_op jit(solution)/shard_map/all_gather | solution.py:114
  871.8 38.1 %all-reduce.17 = f32[64,128]{1,0:T(8,128)S(1)} all-reduce(f32[64,128]{1,0:T(8,128)S(1)} %scatter_custom_fusion.14), channel_id=9, replica_groups=mesh['mat'=4,'frac'=8] {'frac'}, use_global_device_ids=true, to_apply=%region_49.50.clone | all-reduce | flops 8192 | bytes 65536
  935.2 17.8 %all-reduce.18 = (f32[]{:T(128)}, f32[]{:T(128)}) all-reduce(f32[]{:T(128)} %get-tuple-element.28, f32[]{:T(128)} %get-tuple-element.27), channel_id=1, replica_groups=mesh['mat'=4,'frac'=8] {'frac'}, use_global_device_ids=true, to_apply=%region_47.48 | all-reduce | flops 2 | bytes 16 | tf_op jit(solution)/shard_map/psum | solution.py:127
  (229 shorter events, 229.9 us)
Async XLA Ops:
  2.3 498.6 %collective-permute-start = (f32[64,256]{1,0:T(8,128)}, f32[64,256]{1,0:T(8,128)S(1)}, u32[]{:S(2)}, u32[]{:S(2)}) collective-permute-start(f32[64,256]{1,0:T(8,128)} %slice_bitcast_fusion.7), channel_id=1, source_target_pairs={{0,8},{8,16},{16,24},{1,9},{9,17},{17,25},{2,10},{10,18},{18,26},{... | collective-permute-start | bytes 196616 | tf_op jit(solution)/shard_map/ppermute | solution.py:15
  5.7 480.3 %collective-permute-start.1 = (f32[16,256]{1,0:T(8,128)S(1)}, f32[16,256]{1,0:T(8,128)S(1)}, u32[]{:S(2)}, u32[]{:S(2)}) collective-permute-start(f32[16,256]{1,0:T(8,128)S(1)} %bitcast.415), channel_id=1, source_target_pairs={{0,1},{1,2},{2,3},{3,4},{4,5},{5,6},{6,7},{8,9},{9,10},{10,11},{11... | collective-permute-start | bytes 49160 | tf_op jit(solution)/shard_map/ppermute | solution.py:15
  11.5 485.1 %collective-permute-start.3 = (f32[1,64,256]{2,1,0:T(8,128)}, f32[1,64,256]{2,1,0:T(8,128)S(1)}, u32[]{:S(2)}, u32[]{:S(2)}) collective-permute-start(f32[1,64,256]{2,1,0:T(8,128)} %get-tuple-element.72), channel_id=1, source_target_pairs={{0,8},{8,16},{16,24},{1,9},{9,17},{17,25},{2,10},{10,18},{18,26},{... | collective-permute-start | bytes 196616 | tf_op jit(solution)/shard_map/ppermute | solution.py:23
  14.9 481.9 %collective-permute-start.2 = (f32[1,64,256]{2,1,0:T(8,128)}, f32[1,64,256]{2,1,0:T(8,128)S(1)}, u32[]{:S(2)}, u32[]{:S(2)}) collective-permute-start(f32[1,64,256]{2,1,0:T(8,128)} %get-tuple-element.71), channel_id=1, source_target_pairs={{8,0},{16,8},{24,16},{9,1},{17,9},{25,17},{10,2},{18,10},{26,18},{... | collective-permute-start | bytes 196616 | tf_op jit(solution)/shard_map/ppermute | solution.py:26
  23.1 47.8 %all-to-all-start = ((s32[32,1,32]{2,1,0:T(1,128)}), s32[32,1,32]{2,1,0:T(1,128)S(1)}, u32[]{:S(2)}, u32[]{:S(2)}) async-start(s32[32,1,32]{2,1,0:T(1,128)} %all_to_all.30), calls=%async_computation | async-start | bytes 32768 | tf_op jit(solution)/shard_map/all_to_all | solution.py:110
  77.9 47.4 %all-to-all-start.1 = ((f32[32,1,32]{2,1,0:T(1,128)}), f32[32,1,32]{2,1,0:T(1,128)S(1)}, u32[]{:S(2)}, u32[]{:S(2)}) async-start(f32[32,1,32]{2,1,0:T(1,128)} %all_to_all.32), calls=%async_computation.1 | async-start | bytes 32768 | tf_op jit(solution)/shard_map/all_to_all | solution.py:153
  125.3 361.5 %copy-start.23 = (s32[1024]{0:T(1024)}, s32[1024]{0:T(1024)S(1)}, u32[]{:S(2)}) copy-start(s32[1024]{0:T(1024)S(1)} %reshape.528) | copy-start | bytes 12292
  135.5 350.6 %all-to-all-start.2 = ((f32[32,1,32]{2,1,0:T(1,128)}), f32[32,1,32]{2,1,0:T(1,128)S(1)}, u32[]{:S(2)}, u32[]{:S(2)}) async-start(f32[32,1,32]{2,1,0:T(1,128)} %all_to_all.34), calls=%async_computation.2 | async-start | bytes 32768 | tf_op jit(solution)/shard_map/all_to_all | solution.py:169
  497.8 7.7 collective-permute-start.5
  499.5 5.9 collective-permute-start.4
  513.3 6.2 collective-permute-start.6
  514.6 4.9 collective-permute-start.7
  519.5 48.6 %collective-permute-start.9 = (f32[18,1,256]{2,1,0:T(1,128)S(1)}, f32[18,1,256]{2,1,0:T(1,128)S(1)}, u32[]{:S(2)}, u32[]{:S(2)}) collective-permute-start(f32[18,1,256]{2,1,0:T(1,128)S(1)} %get-tuple-element.62), channel_id=1, source_target_pairs={{0,1},{1,2},{2,3},{3,4},{4,5},{5,6},{6,7},{8,9},{9,10},{10,11},{11... | collective-permute-start | bytes 55304 | tf_op jit(solution)/shard_map/ppermute | solution.py:23
  524.0 44.0 %collective-permute-start.8 = (f32[18,1,256]{2,1,0:T(1,128)S(1)}, f32[18,1,256]{2,1,0:T(1,128)S(1)}, u32[]{:S(2)}, u32[]{:S(2)}) collective-permute-start(f32[18,1,256]{2,1,0:T(1,128)S(1)} %get-tuple-element.61), channel_id=1, source_target_pairs={{1,0},{2,1},{3,2},{4,3},{5,4},{6,5},{7,6},{9,8},{10,9},{11,10},{12... | collective-permute-start | bytes 55304 | tf_op jit(solution)/shard_map/ppermute | solution.py:26
  584.8 9.7 all-to-all-start.3
  588.3 278.8 %collective-permute-start.10 = (f32[1,64,256]{2,1,0:T(8,128)S(1)}, f32[1,64,256]{2,1,0:T(8,128)S(1)}, u32[]{:S(2)}, u32[]{:S(2)}) collective-permute-start(f32[1,64,256]{2,1,0:T(8,128)S(1)} %get-tuple-element.68), channel_id=1, source_target_pairs={{8,0},{16,8},{24,16},{9,1},{17,9},{25,17},{10,2},{18,10},{26,18},{... | collective-permute-start | bytes 196616 | tf_op jit(solution)/shard_map/ppermute | solution.py:26
  589.6 277.5 %collective-permute-start.11 = (f32[1,64,256]{2,1,0:T(8,128)S(1)}, f32[1,64,256]{2,1,0:T(8,128)S(1)}, u32[]{:S(2)}, u32[]{:S(2)}) collective-permute-start(f32[1,64,256]{2,1,0:T(8,128)S(1)} %get-tuple-element.67), channel_id=1, source_target_pairs={{0,8},{8,16},{16,24},{1,9},{9,17},{17,25},{2,10},{10,18},{18,26},{... | collective-permute-start | bytes 196616 | tf_op jit(solution)/shard_map/ppermute | solution.py:23
  604.3 305.6 %all-to-all-start.4 = ((f32[32,1,32]{2,1,0:T(1,128)}), f32[32,1,32]{2,1,0:T(1,128)S(1)}, u32[]{:S(2)}, u32[]{:S(2)}) async-start(f32[32,1,32]{2,1,0:T(1,128)} %all_to_all.38), calls=%async_computation.4 | async-start | bytes 32768 | tf_op jit(solution)/shard_map/all_to_all | solution.py:169
  867.1 53.6 %collective-permute-start.13 = (f32[18,1,256]{2,1,0:T(1,128)S(1)}, f32[18,1,256]{2,1,0:T(1,128)S(1)}, u32[]{:S(2)}, u32[]{:S(2)}) collective-permute-start(f32[18,1,256]{2,1,0:T(1,128)S(1)} %get-tuple-element.60), channel_id=1, source_target_pairs={{0,1},{1,2},{2,3},{3,4},{4,5},{5,6},{6,7},{8,9},{9,10},{10,11},{11... | collective-permute-start | bytes 55304 | tf_op jit(solution)/shard_map/ppermute | solution.py:23
  868.4 52.3 %collective-permute-start.12 = (f32[18,1,256]{2,1,0:T(1,128)S(1)}, f32[18,1,256]{2,1,0:T(1,128)S(1)}, u32[]{:S(2)}, u32[]{:S(2)}) collective-permute-start(f32[18,1,256]{2,1,0:T(1,128)S(1)} %get-tuple-element.59), channel_id=1, source_target_pairs={{1,0},{2,1},{3,2},{4,3},{5,4},{6,5},{7,6},{9,8},{10,9},{11,10},{12... | collective-permute-start | bytes 55304 | tf_op jit(solution)/shard_map/ppermute | solution.py:26
  930.3 26.8 %collective-permute-start.14 = (f32[1,64,256]{2,1,0:T(8,128)S(1)}, f32[1,64,256]{2,1,0:T(8,128)S(1)}, u32[]{:S(2)}, u32[]{:S(2)}) collective-permute-start(f32[1,64,256]{2,1,0:T(8,128)S(1)} %get-tuple-element.66), channel_id=1, source_target_pairs={{8,0},{16,8},{24,16},{9,1},{17,9},{25,17},{10,2},{18,10},{26,18},{... | collective-permute-start | bytes 196616 | tf_op jit(solution)/shard_map/ppermute | solution.py:26
  931.6 25.5 %collective-permute-start.15 = (f32[1,64,256]{2,1,0:T(8,128)S(1)}, f32[1,64,256]{2,1,0:T(8,128)S(1)}, u32[]{:S(2)}, u32[]{:S(2)}) collective-permute-start(f32[1,64,256]{2,1,0:T(8,128)S(1)} %get-tuple-element.65), channel_id=1, source_target_pairs={{0,8},{8,16},{16,24},{1,9},{9,17},{17,25},{2,10},{10,18},{18,26},{... | collective-permute-start | bytes 196616 | tf_op jit(solution)/shard_map/ppermute | solution.py:23
  958.0 5.8 collective-permute-start.17
  962.0 5.7 collective-permute-start.16
  (26 other events, 1407.7 us)
where the time goes:
time: 987 us; the launch traced here: 977 us
  blocking collectives  725 us (73%)
  other arithmetic  78.4 us (8%)
  starting transfers between devices  61.4 us (6%)
  local copies, waits for them, and re-layouts  60.8 us (6%)
  matrix products  23.6 us (2%)
  between operations  22 us (2%)
    unnamed x8, blocking collectives  291 us
    all_gather x6, blocking collectives, fracture_apply(): whole = lax.all_gather(vector, 'frac', axis=0, tiled=True)  184 us
    psum x6, blocking collectives, two_products(): lax.psum((jnp.sum(residual * residual), jnp.sum(residual * image)), 'frac')  107 us
    psum x2, blocking collectives, body(): summed = lax.psum(landed, ('mat', 'frac'))  81.6 us
    all_gather x2, blocking collectives, body(): fracture_whole = lax.all_gather(fracture, 'frac', axis=0, tiled=True)  61.7 us
    select_n x4, other arithmetic, relax(): return jnp.where(inside, updated, 0.0)  33.9 us
    ppermute x8, starting transfers between devices, with_halo(): lax.ppermute(lax.slice_in_dim(block, block.shape[dim] - width, None, axis...  24 us
  transfers between devices with their start and end apart: 23, of which 2 were waited for; matrix products, arithmetic and copies ran while one was open for 12% of the time, Pallas kernels for 0%

commit v1 on v0

--- a/solution.py
+++ b/solution.py
@@ -111,7 +111,14 @@
     asked_safe = jnp.minimum(asked, cells - 1)
 
     def fracture_apply(vector):
-        whole = lax.all_gather(vector, "frac", axis=0, tiled=True)
+        ring = [vector]
+        for hop in range(7):
+            ring.append(lax.ppermute(ring[-1], "frac", [(dev, (dev + 1) % 8) for dev in range(8)]))
+        whole = jnp.roll(
+            jnp.concatenate(ring[::-1], axis=0),
+            (lax.axis_index("frac") + 1) * ring[0].shape[0],
+            axis=0,
+        )
         blocks = whole.reshape(-1, size_b)
         forward = jnp.einsum(
             "rtij,rtj->ri", tiles, blocks[tile_cols], precision=lax.Precision.HIGHEST

time: 987 us -> 1040 us (1.054)
  blocking collectives: 725 us -> 550 us
  waiting for transfers between devices: 5.71 us -> 179 us
  starting transfers between devices: 61.4 us -> 97.7 us
    all_gather x6 -> x0, blocking collectives: 184 us -> none  [fracture_apply(): whole = lax.all_gather(vector, 'frac', axis=0, tiled=True)]
    ppermute x0 -> x56, waiting for transfers between devices: none -> 157 us  [fracture_apply(): lax.ppermute(ring[-1], 'frac', [(dev, (dev + 1) % 8) for dev in range(8)])]
    ppermute x0 -> x56, starting transfers between devices: none -> 31.9 us  [fracture_apply(): lax.ppermute(ring[-1], 'frac', [(dev, (dev + 1) % 8) for dev in range(8)])]
  transfers between devices with their start and end apart: 23 -> 79, of which waited for: 2 -> 40; matrix products, arithmetic and copies ran while one was open for 12% -> 12% of each run, Pallas kernels for 0% -> 0%
where the time goes in v1:
time: 1040 us; the launch traced here: 1030 us
  blocking collectives  550 us (53%)
  waiting for transfers between devices  179 us (17%)
  starting transfers between devices  97.7 us (9%)
  other arithmetic  83.1 us (8%)
  local copies, waits for them, and re-layouts  69.2 us (7%)
  matrix products  24.2 us (2%)
  between operations  22.5 us (2%)
    unnamed x8, blocking collectives  300 us
    ppermute x56, waiting for transfers between devices, fracture_apply(): lax.ppermute(ring[-1], 'frac', [(dev, (dev + 1) % 8) for dev in range(8)])  157 us
    psum x6, blocking collectives, two_products(): lax.psum((jnp.sum(residual * residual), jnp.sum(residual * image)), 'frac')  111 us
    psum x2, blocking collectives, body(): summed = lax.psum(landed, ('mat', 'frac'))  78.5 us
    all_gather x2, blocking collectives, body(): fracture_whole = lax.all_gather(fracture, 'frac', axis=0, tiled=True)  61.3 us
    select_n x4, other arithmetic, relax(): return jnp.where(inside, updated, 0.0)  34.5 us
    ppermute x56, starting transfers between devices, fracture_apply(): lax.ppermute(ring[-1], 'frac', [(dev, (dev + 1) % 8) for dev in range(8)])  31.9 us
    ppermute x8, starting transfers between devices, with_halo(): lax.ppermute(lax.slice_in_dim(block, block.shape[dim] - width, None, axis...  23.8 us
  transfers between devices with their start and end apart: 79, of which 40 were waited for; matrix products, arithmetic and copies ran while one was open for 12% of the time, Pallas kernels for 0%

profile of v1, /device:TPU:0, one launch (start us, length us, event | category | flops | bytes accessed | tf_op | source)
XLA Modules:
  0.0 1025.3 jit_solution(16130938049279696798)
XLA Ops:
  7.7 7.3 all-to-all-start
  21.7 35.8 %all-reduce.10 = f32[64,128]{1,0:T(8,128)S(1)} all-reduce(f32[64,128]{1,0:T(8,128)S(1)} %scatter_custom_fusion.4), channel_id=2, replica_groups=mesh['mat'=4,'frac'=8] {'frac'}, use_global_device_ids=true, to_apply=%region_9.11.clone | all-reduce | flops 8192 | bytes 65536
  87.2 30.7 %all_gather.6 = f32[8192]{0:T(1024)S(1)} all-gather(f32[1024]{0:T(1024)S(1)} %copy-done.8), channel_id=1, replica_groups=mesh['mat'=4,'frac'=8] {'frac'}, dimensions={0}, use_global_device_ids=true | all-gather | bytes 36864 | tf_op jit(solution)/shard_map/all_gather | solution.py:164
  132.1 40.1 %psum.98 = f32[8192]{0:T(1024)S(1)} all-reduce(f32[8192]{0:T(1024)S(1)} %scatter_custom_fusion.3), channel_id=1, replica_groups=mesh['mat'=4,'frac'=8] {'mat','frac'}, use_global_device_ids=true, to_apply=%region_7.8 | all-reduce | flops 8192 | bytes 65536 | tf_op jit(solution)/shard_map/psum | solution.py:167
  212.7 37.9 %all-reduce.11 = f32[64,128]{1,0:T(8,128)S(1)} all-reduce(f32[64,128]{1,0:T(8,128)S(1)} %scatter_custom_fusion.5), channel_id=3, replica_groups=mesh['mat'=4,'frac'=8] {'frac'}, use_global_device_ids=true, to_apply=%region_13.15.clone | all-reduce | flops 8192 | bytes 65536
  253.7 17.8 %all-reduce.23 = (f32[]{:T(128)}, f32[]{:T(128)}) all-reduce(f32[]{:T(128)} %get-tuple-element.39, f32[]{:T(128)} %get-tuple-element.38), channel_id=1, replica_groups=mesh['mat'=4,'frac'=8] {'frac'}, use_global_device_ids=true, to_apply=%region_11.13 | all-reduce | flops 2 | bytes 16 | tf_op jit(solution)/shard_map/psum | solution.py:134
  310.8 37.6 %all-reduce.12 = f32[64,128]{1,0:T(8,128)S(1)} all-reduce(f32[64,128]{1,0:T(8,128)S(1)} %scatter_custom_fusion.6), channel_id=4, replica_groups=mesh['mat'=4,'frac'=8] {'frac'}, use_global_device_ids=true, to_apply=%region_19.21.clone | all-reduce | flops 8192 | bytes 65536
  354.9 17.8 %all-reduce.22 = (f32[]{:T(128)}, f32[]{:T(128)}) all-reduce(f32[]{:T(128)} %get-tuple-element.37, f32[]{:T(128)} %get-tuple-element.36), channel_id=1, replica_groups=mesh['mat'=4,'frac'=8] {'frac'}, use_global_device_ids=true, to_apply=%region_17.19 | all-reduce | flops 2 | bytes 16 | tf_op jit(solution)/shard_map/psum | solution.py:134
  395.4 7.2 scatter_custom_fusion.2
  430.4 37.9 %all-reduce.13 = f32[64,128]{1,0:T(8,128)S(1)} all-reduce(f32[64,128]{1,0:T(8,128)S(1)} %scatter_custom_fusion.7), channel_id=5, replica_groups=mesh['mat'=4,'frac'=8] {'frac'}, use_global_device_ids=true, to_apply=%region_25.27.clone | all-reduce | flops 8192 | bytes 65536
  471.4 17.8 %all-reduce.21 = (f32[]{:T(128)}, f32[]{:T(128)}) all-reduce(f32[]{:T(128)} %get-tuple-element.35, f32[]{:T(128)} %get-tuple-element.34), channel_id=1, replica_groups=mesh['mat'=4,'frac'=8] {'frac'}, use_global_device_ids=true, to_apply=%region_23.25 | all-reduce | flops 2 | bytes 16 | tf_op jit(solution)/shard_map/psum | solution.py:134
  510.2 7.9 broadcast_select_fusion.1
  530.9 37.6 %all-reduce.14 = f32[64,128]{1,0:T(8,128)S(1)} all-reduce(f32[64,128]{1,0:T(8,128)S(1)} %scatter_custom_fusion.11), channel_id=6, replica_groups=mesh['mat'=4,'frac'=8] {'frac'}, use_global_device_ids=true, to_apply=%region_33.35.clone | all-reduce | flops 8192 | bytes 65536
  568.5 30.6 %all_gather.7 = f32[8192]{0:T(1024)S(1)} all-gather(f32[1024]{0:T(1024)S(1)} %multiply_add_fusion.1), channel_id=1, replica_groups=mesh['mat'=4,'frac'=8] {'frac'}, dimensions={0}, use_global_device_ids=true | all-gather | bytes 36864 | tf_op jit(solution)/shard_map/all_gather | solution.py:164
  614.2 8.4 fusion.75
  649.0 38.3 %psum.105 = f32[8192]{0:T(1024)S(1)} all-reduce(f32[8192]{0:T(1024)S(1)} %scatter_custom_fusion.10), channel_id=1, replica_groups=mesh['mat'=4,'frac'=8] {'mat','frac'}, use_global_device_ids=true, to_apply=%region_31.33 | all-reduce | flops 8192 | bytes 65536 | tf_op jit(solution)/shard_map/psum | solution.py:167
  725.2 37.6 %all-reduce.15 = f32[64,128]{1,0:T(8,128)S(1)} all-reduce(f32[64,128]{1,0:T(8,128)S(1)} %scatter_custom_fusion.12), channel_id=7, replica_groups=mesh['mat'=4,'frac'=8] {'frac'}, use_global_device_ids=true, to_apply=%region_37.39.clone | all-reduce | flops 8192 | bytes 65536
  766.0 17.8 %all-reduce.20 = (f32[]{:T(128)}, f32[]{:T(128)}) all-reduce(f32[]{:T(128)} %get-tuple-element.33, f32[]{:T(128)} %get-tuple-element.32), channel_id=1, replica_groups=mesh['mat'=4,'frac'=8] {'frac'}, use_global_device_ids=true, to_apply=%region_35.37 | all-reduce | flops 2 | bytes 16 | tf_op jit(solution)/shard_map/psum | solution.py:134
  824.6 37.9 %all-reduce.16 = f32[64,128]{1,0:T(8,128)S(1)} all-reduce(f32[64,128]{1,0:T(8,128)S(1)} %scatter_custom_fusion.13), channel_id=8, replica_groups=mesh['mat'=4,'frac'=8] {'frac'}, use_global_device_ids=true, to_apply=%region_43.45.clone | all-reduce | flops 8192 | bytes 65536
  865.7 17.8 %all-reduce.19 = (f32[]{:T(128)}, f32[]{:T(128)}) all-reduce(f32[]{:T(128)} %get-tuple-element.31, f32[]{:T(128)} %get-tuple-element.30), channel_id=1, replica_groups=mesh['mat'=4,'frac'=8] {'frac'}, use_global_device_ids=true, to_apply=%region_41.43 | all-reduce | flops 2 | bytes 16 | tf_op jit(solution)/shard_map/psum | solution.py:134
  924.4 37.6 %all-reduce.17 = f32[64,128]{1,0:T(8,128)S(1)} all-reduce(f32[64,128]{1,0:T(8,128)S(1)} %scatter_custom_fusion.14), channel_id=9, replica_groups=mesh['mat'=4,'frac'=8] {'frac'}, use_global_device_ids=true, to_apply=%region_49.51.clone | all-reduce | flops 8192 | bytes 65536
  962.0 8.8 broadcast_select_fusion
  982.3 21.5 %all-reduce.18 = (f32[]{:T(128)}, f32[]{:T(128)}) all-reduce(f32[]{:T(128)} %get-tuple-element.29, f32[]{:T(128)} %get-tuple-element.28), channel_id=1, replica_groups=mesh['mat'=4,'frac'=8] {'frac'}, use_global_device_ids=true, to_apply=%region_47.49 | all-reduce | flops 2 | bytes 16 | tf_op jit(solution)/shard_map/psum | solution.py:134
  1015.7 9.4 fusion.74
  (418 shorter events, 403.8 us)
Async XLA Ops:
  7.7 51.8 %all-to-all-start = ((s32[32,1,32]{2,1,0:T(1,128)}), s32[32,1,32]{2,1,0:T(1,128)S(1)}, u32[]{:S(2)}, u32[]{:S(2)}) async-start(s32[32,1,32]{2,1,0:T(1,128)} %all_to_all.30), calls=%async_computation | async-start | bytes 32768 | tf_op jit(solution)/shard_map/all_to_all | solution.py:110
  15.0 44.4 %collective-permute-start.10 = (f32[1024]{0:T(1024)}, f32[1024]{0:T(1024)S(1)}, u32[]{:S(2)}, u32[]{:S(2)}) collective-permute-start(f32[1024]{0:T(1024)} %param.31), channel_id=1, source_target_pairs={{0,1},{1,2},{2,3},{3,4},{4,5},{5,6},{6,7},{7,0},{8,9},{9,10},{10,1... | collective-permute-start | bytes 12296 | tf_op jit(solution)/shard_map/ppermute | solution.py:116
  79.0 43.2 %all-to-all-start.1 = ((f32[32,1,32]{2,1,0:T(1,128)}), f32[32,1,32]{2,1,0:T(1,128)S(1)}, u32[]{:S(2)}, u32[]{:S(2)}) async-start(f32[32,1,32]{2,1,0:T(1,128)} %all_to_all.32), calls=%async_computation.1 | async-start | bytes 32768 | tf_op jit(solution)/shard_map/all_to_all | solution.py:160
  85.3 40.4 %collective-permute-start.14 = (f32[1024]{0:T(1024)S(1)}, f32[1024]{0:T(1024)S(1)}, u32[]{:S(2)}, u32[]{:S(2)}) collective-permute-start(f32[1024]{0:T(1024)S(1)} %collective-permute-done.13), channel_id=1, source_target_pairs={{0,1},{1,2},{2,3},{3,4},{4,5},{5,6},{6,7},{7,0},{8,9},{9,10},{10,1... | collective-permute-start | bytes 12296 | tf_op jit(solution)/shard_map/ppermute | solution.py:116
  132.1 40.1 %collective-permute-start.16 = (f32[1024]{0:T(1024)S(1)}, f32[1024]{0:T(1024)S(1)}, u32[]{:S(2)}, u32[]{:S(2)}) collective-permute-start(f32[1024]{0:T(1024)S(1)} %collective-permute-done.15), channel_id=1, source_target_pairs={{0,1},{1,2},{2,3},{3,4},{4,5},{5,6},{6,7},{7,0},{8,9},{9,10},{10,1... | collective-permute-start | bytes 12296 | tf_op jit(solution)/shard_map/ppermute | solution.py:116
  212.7 37.9 %collective-permute-start.23 = (f32[1024]{0:T(1024)S(1)}, f32[1024]{0:T(1024)S(1)}, u32[]{:S(2)}, u32[]{:S(2)}) collective-permute-start(f32[1024]{0:T(1024)S(1)} %collective-permute-done.22), channel_id=1, source_target_pairs={{0,1},{1,2},{2,3},{3,4},{4,5},{5,6},{6,7},{7,0},{8,9},{9,10},{10,1... | collective-permute-start | bytes 12296 | tf_op jit(solution)/shard_map/ppermute | solution.py:116
  280.0 220.1 %collective-permute-start = (f32[64,256]{1,0:T(8,128)S(1)}, f32[64,256]{1,0:T(8,128)S(1)}, u32[]{:S(2)}, u32[]{:S(2)}) collective-permute-start(f32[64,256]{1,0:T(8,128)S(1)} %slice_bitcast_fusion.7), channel_id=1, source_target_pairs={{0,8},{8,16},{16,24},{1,9},{9,17},{17,25},{2,10},{10,18},{18,26},{... | collective-permute-start | bytes 196616 | tf_op jit(solution)/shard_map/ppermute | solution.py:15
  282.3 108.0 %collective-permute-start.1 = (f32[16,256]{1,0:T(8,128)S(1)}, f32[16,256]{1,0:T(8,128)}, u32[]{:S(2)}, u32[]{:S(2)}) collective-permute-start(f32[16,256]{1,0:T(8,128)S(1)} %bitcast.415), channel_id=1, source_target_pairs={{0,1},{1,2},{2,3},{3,4},{4,5},{5,6},{6,7},{8,9},{9,10},{10,11},{11... | collective-permute-start | bytes 49160 | tf_op jit(solution)/shard_map/ppermute | solution.py:15
  286.2 119.9 %collective-permute-start.3 = (f32[1,64,256]{2,1,0:T(8,128)}, f32[1,64,256]{2,1,0:T(8,128)S(1)}, u32[]{:S(2)}, u32[]{:S(2)}) collective-permute-start(f32[1,64,256]{2,1,0:T(8,128)} %get-tuple-element.73), channel_id=1, source_target_pairs={{0,8},{8,16},{16,24},{1,9},{9,17},{17,25},{2,10},{10,18},{18,26},{... | collective-permute-start | bytes 196616 | tf_op jit(solution)/shard_map/ppermute | solution.py:23
  290.2 127.5 %collective-permute-start.2 = (f32[1,64,256]{2,1,0:T(8,128)}, f32[1,64,256]{2,1,0:T(8,128)S(1)}, u32[]{:S(2)}, u32[]{:S(2)}) collective-permute-start(f32[1,64,256]{2,1,0:T(8,128)} %get-tuple-element.72), channel_id=1, source_target_pairs={{8,0},{16,8},{24,16},{9,1},{17,9},{25,17},{10,2},{18,10},{26,18},{... | collective-permute-start | bytes 196616 | tf_op jit(solution)/shard_map/ppermute | solution.py:26
  310.8 37.6 %collective-permute-start.30 = (f32[1024]{0:T(1024)}, f32[1024]{0:T(1024)S(1)}, u32[]{:S(2)}, u32[]{:S(2)}) collective-permute-start(f32[1024]{0:T(1024)} %collective-permute-done.29), channel_id=1, source_target_pairs={{0,1},{1,2},{2,3},{3,4},{4,5},{5,6},{6,7},{7,0},{8,9},{9,10},{10,1... | collective-permute-start | bytes 12296 | tf_op jit(solution)/shard_map/ppermute | solution.py:116
  430.4 37.9 %collective-permute-start.37 = (f32[1024]{0:T(1024)S(1)}, f32[1024]{0:T(1024)S(1)}, u32[]{:S(2)}, u32[]{:S(2)}) collective-permute-start(f32[1024]{0:T(1024)S(1)} %collective-permute-done.36), channel_id=1, source_target_pairs={{0,1},{1,2},{2,3},{3,4},{4,5},{5,6},{6,7},{7,0},{8,9},{9,10},{10,1... | collective-permute-start | bytes 12296 | tf_op jit(solution)/shard_map/ppermute | solution.py:116
  519.6 84.1 %collective-permute-start.6 = (f32[1,64,256]{2,1,0:T(8,128)S(1)}, f32[1,64,256]{2,1,0:T(8,128)S(1)}, u32[]{:S(2)}, u32[]{:S(2)}) collective-permute-start(f32[1,64,256]{2,1,0:T(8,128)S(1)} %get-tuple-element.71), channel_id=1, source_target_pairs={{8,0},{16,8},{24,16},{9,1},{17,9},{25,17},{10,2},{18,10},{26,18},{... | collective-permute-start | bytes 196616 | tf_op jit(solution)/shard_map/ppermute | solution.py:26
  520.9 82.8 %collective-permute-start.7 = (f32[1,64,256]{2,1,0:T(8,128)S(1)}, f32[1,64,256]{2,1,0:T(8,128)S(1)}, u32[]{:S(2)}, u32[]{:S(2)}) collective-permute-start(f32[1,64,256]{2,1,0:T(8,128)S(1)} %get-tuple-element.70), channel_id=1, source_target_pairs={{0,8},{8,16},{16,24},{1,9},{9,17},{17,25},{2,10},{10,18},{18,26},{... | collective-permute-start | bytes 196616 | tf_op jit(solution)/shard_map/ppermute | solution.py:23
  530.9 37.6 %collective-permute-start.51 = (f32[1024]{0:T(1024)S(1)}, f32[1024]{0:T(1024)S(1)}, u32[]{:S(2)}, u32[]{:S(2)}) collective-permute-start(f32[1024]{0:T(1024)S(1)} %collective-permute-done.50), channel_id=1, source_target_pairs={{0,1},{1,2},{2,3},{3,4},{4,5},{5,6},{6,7},{7,0},{8,9},{9,10},{10,1... | collective-permute-start | bytes 12296 | tf_op jit(solution)/shard_map/ppermute | solution.py:116
  725.2 37.6 %collective-permute-start.59 = (f32[1024]{0:T(1024)S(1)}, f32[1024]{0:T(1024)S(1)}, u32[]{:S(2)}, u32[]{:S(2)}) collective-permute-start(f32[1024]{0:T(1024)S(1)} %collective-permute-done.58), channel_id=1, source_target_pairs={{0,1},{1,2},{2,3},{3,4},{4,5},{5,6},{6,7},{7,0},{8,9},{9,10},{10,1... | collective-permute-start | bytes 12296 | tf_op jit(solution)/shard_map/ppermute | solution.py:116
  811.3 100.8 %collective-permute-start.38 = (f32[1,64,256]{2,1,0:T(8,128)S(1)}, f32[1,64,256]{2,1,0:T(8,128)S(1)}, u32[]{:S(2)}, u32[]{:S(2)}) collective-permute-start(f32[1,64,256]{2,1,0:T(8,128)S(1)} %get-tuple-element.69), channel_id=1, source_target_pairs={{8,0},{16,8},{24,16},{9,1},{17,9},{25,17},{10,2},{18,10},{26,18},{... | collective-permute-start | bytes 196616 | tf_op jit(solution)/shard_map/ppermute | solution.py:26
  812.6 99.5 %collective-permute-start.39 = (f32[1,64,256]{2,1,0:T(8,128)S(1)}, f32[1,64,256]{2,1,0:T(8,128)S(1)}, u32[]{:S(2)}, u32[]{:S(2)}) collective-permute-start(f32[1,64,256]{2,1,0:T(8,128)S(1)} %get-tuple-element.68), channel_id=1, source_target_pairs={{0,8},{8,16},{16,24},{1,9},{9,17},{17,25},{2,10},{10,18},{18,26},{... | collective-permute-start | bytes 196616 | tf_op jit(solution)/shard_map/ppermute | solution.py:23
  824.6 37.9 %collective-permute-start.66 = (f32[1024]{0:T(1024)S(1)}, f32[1024]{0:T(1024)S(1)}, u32[]{:S(2)}, u32[]{:S(2)}) collective-permute-start(f32[1024]{0:T(1024)S(1)} %collective-permute-done.65), channel_id=1, source_target_pairs={{0,1},{1,2},{2,3},{3,4},{4,5},{5,6},{6,7},{7,0},{8,9},{9,10},{10,1... | collective-permute-start | bytes 12296 | tf_op jit(solution)/shard_map/ppermute | solution.py:116
  913.0 49.0 %collective-permute-start.41 = (f32[18,1,256]{2,1,0:T(1,128)S(1)}, f32[18,1,256]{2,1,0:T(1,128)S(1)}, u32[]{:S(2)}, u32[]{:S(2)}) collective-permute-start(f32[18,1,256]{2,1,0:T(1,128)S(1)} %get-tuple-element.61), channel_id=1, source_target_pairs={{0,1},{1,2},{2,3},{3,4},{4,5},{5,6},{6,7},{8,9},{9,10},{10,11},{11... | collective-permute-start | bytes 55304 | tf_op jit(solution)/shard_map/ppermute | solution.py:23
  916.6 45.4 %collective-permute-start.40 = (f32[18,1,256]{2,1,0:T(1,128)S(1)}, f32[18,1,256]{2,1,0:T(1,128)S(1)}, u32[]{:S(2)}, u32[]{:S(2)}) collective-permute-start(f32[18,1,256]{2,1,0:T(1,128)S(1)} %get-tuple-element.60), channel_id=1, source_target_pairs={{1,0},{2,1},{3,2},{4,3},{5,4},{6,5},{7,6},{9,8},{10,9},{11,10},{12... | collective-permute-start | bytes 55304 | tf_op jit(solution)/shard_map/ppermute | solution.py:26
  924.3 37.6 %collective-permute-start.71 = (f32[1024]{0:T(1024)S(1)}, f32[1024]{0:T(1024)S(1)}, u32[]{:S(2)}, u32[]{:S(2)}) collective-permute-start(f32[1024]{0:T(1024)S(1)} %collective-permute-done.70), channel_id=1, source_target_pairs={{0,1},{1,2},{2,3},{3,4},{4,5},{5,6},{6,7},{7,0},{8,9},{9,10},{10,1... | collective-permute-start | bytes 12296 | tf_op jit(solution)/shard_map/ppermute | solution.py:116
  971.9 35.8 %collective-permute-start.42 = (f32[1,64,256]{2,1,0:T(8,128)S(1)}, f32[1,64,256]{2,1,0:T(8,128)S(1)}, u32[]{:S(2)}, u32[]{:S(2)}) collective-permute-start(f32[1,64,256]{2,1,0:T(8,128)S(1)} %get-tuple-element.67), channel_id=1, source_target_pairs={{8,0},{16,8},{24,16},{9,1},{17,9},{25,17},{10,2},{18,10},{26,18},{... | collective-permute-start | bytes 196616 | tf_op jit(solution)/shard_map/ppermute | solution.py:26
  973.2 34.5 %collective-permute-start.43 = (f32[1,64,256]{2,1,0:T(8,128)S(1)}, f32[1,64,256]{2,1,0:T(8,128)S(1)}, u32[]{:S(2)}, u32[]{:S(2)}) collective-permute-start(f32[1,64,256]{2,1,0:T(8,128)S(1)} %get-tuple-element.66), channel_id=1, source_target_pairs={{0,8},{8,16},{16,24},{1,9},{9,17},{17,25},{2,10},{10,18},{18,26},{... | collective-permute-start | bytes 196616 | tf_op jit(solution)/shard_map/ppermute | solution.py:23
  (88 other events, 1965.1 us)
